TPU v7x, 16 devices: a whole 2x2x2 slice. The times are simulated.
16 devices in a mesh: local: 4 (over z, y), data: 4 (over x, core).
Axes of the slice: x: 2, y: 2, z: 2, core: 2. Of those that a mesh axis runs over, the one named last changes fastest.
Arguments:
- tokens: bfloat16 [2, 32768, 1024], P(None, ('local', 'data'))
- cotangent: bfloat16 [2, 32768, 1024], P(None, ('local', 'data'))
- w_up: bfloat16 [2, 1024, 4096], P(None, ('local', 'data'))
- w_down: bfloat16 [2, 4096, 1024], P(None, ('local', 'data'))
Outputs:
- output 1: bfloat16 [2, 32768, 1024], P(None, ('local', 'data'))
- output 2: bfloat16 [2, 32768, 1024], P(None, ('local', 'data'))
- output 3: float32 [2, 1024, 4096], P(None, ('local', 'data'))
- output 4: float32 [2, 4096, 1024], P(None, ('local', 'data'))
All inputs are finite; a program needn't handle non-finite values.
Results may differ from a plain program's by a relative error of at most 0.0130687.
Values are sent between devices in bfloat16 or wider.
A program may use at most 1 GiB of HBM per device.

v0:
```python
import jax
import jax.numpy as jnp
from jax import lax
from jax.sharding import PartitionSpec as P

NORM_EPS = 1e-6
ALL_AXES = ("local", "data")


def norm_f32(x_f32):
    return x_f32 * lax.rsqrt(jnp.mean(x_f32 * x_f32, axis=-1, keepdims=True) + NORM_EPS)


def gelu_f32(pre_f32):
    return jax.nn.gelu(pre_f32, approximate=True)


def layer_forward(x_in, up_mat, down_mat):
    x_f32 = x_in.astype(jnp.float32)
    normed = norm_f32(x_f32).astype(jnp.bfloat16)
    pre_act = jnp.dot(normed, up_mat, preferred_element_type=jnp.float32).astype(jnp.bfloat16)
    hidden = gelu_f32(pre_act.astype(jnp.float32)).astype(jnp.bfloat16)
    x_out = (x_f32 + jnp.dot(hidden, down_mat, preferred_element_type=jnp.float32)).astype(jnp.bfloat16)
    return x_out, normed, pre_act, hidden


def layer_backward(d_out, x_in, normed, pre_act, hidden, up_mat, down_mat):
    d_hidden = jnp.einsum("tm,fm->tf", d_out, down_mat, preferred_element_type=jnp.float32)
    gelu_pull = jax.vjp(gelu_f32, pre_act.astype(jnp.float32))[1]
    d_pre = gelu_pull(d_hidden)[0].astype(jnp.bfloat16)
    d_normed = jnp.einsum("tf,mf->tm", d_pre, up_mat, preferred_element_type=jnp.float32)
    norm_pull = jax.vjp(norm_f32, x_in.astype(jnp.float32))[1]
    d_in = (d_out.astype(jnp.float32) + norm_pull(d_normed)[0]).astype(jnp.bfloat16)
    grad_up = jnp.einsum("tm,tf->mf", normed, d_pre, preferred_element_type=jnp.float32)
    grad_down = jnp.einsum("tf,tm->fm", hidden, d_out, preferred_element_type=jnp.float32)
    return d_in, grad_up, grad_down


def solution(mesh):
    data_size = mesh.shape["data"]

    def body(tokens, cotangent, w_up, w_down):
        layers = w_up.shape[0]
        local_idx = lax.axis_index("local")
        keep_up = w_up.shape[1] * data_size
        keep_down = w_down.shape[1] * data_size
        total_up = [None] * layers
        total_down = [None] * layers
        outs_x = []
        outs_dx = []
        for micro_idx in range(tokens.shape[0]):
            x_cur = tokens[micro_idx]
            saved_acts = []
            for layer_idx in range(layers):
                full_up = lax.all_gather(w_up[layer_idx], ALL_AXES, axis=0, tiled=True)
                full_down = lax.all_gather(w_down[layer_idx], ALL_AXES, axis=0, tiled=True)
                kept_up = lax.dynamic_slice_in_dim(full_up, local_idx * keep_up, keep_up, axis=0)
                kept_down = lax.dynamic_slice_in_dim(full_down, local_idx * keep_down, keep_down, axis=0)
                x_next, normed, pre_act, hidden = layer_forward(x_cur, full_up, full_down)
                saved_acts.append((x_cur, normed, pre_act, hidden, kept_up, kept_down))
                x_cur = x_next
            outs_x.append(x_cur)
            d_cur = cotangent[micro_idx]
            for layer_idx in reversed(range(layers)):
                x_in, normed, pre_act, hidden, kept_up, kept_down = saved_acts[layer_idx]
                full_up = lax.all_gather(kept_up, "local", axis=0, tiled=True)
                full_down = lax.all_gather(kept_down, "local", axis=0, tiled=True)
                d_cur, grad_up, grad_down = layer_backward(d_cur, x_in, normed, pre_act, hidden, full_up, full_down)
                total_up[layer_idx] = grad_up if total_up[layer_idx] is None else total_up[layer_idx] + grad_up
                total_down[layer_idx] = grad_down if total_down[layer_idx] is None else total_down[layer_idx] + grad_down
            outs_dx.append(d_cur)
        shard_up = [lax.psum_scatter(total, ALL_AXES, scatter_dimension=0, tiled=True) for total in total_up]
        shard_down = [lax.psum_scatter(total, ALL_AXES, scatter_dimension=0, tiled=True) for total in total_down]
        return jnp.stack(outs_x), jnp.stack(outs_dx), jnp.stack(shard_up), jnp.stack(shard_down)

    row_spec = P(None, ALL_AXES, None)
    return jax.shard_map(body, mesh=mesh, in_specs=(row_spec, row_spec, row_spec, row_spec), out_specs=(row_spec, row_spec, row_spec, row_spec), check_vma=False)
```

profile of v0, /device:TPU:0, one launch (start us, length us, event | category | flops | bytes accessed | tf_op | source)
XLA Modules:
  0.0 1281.0 jit_solution(5295578659406749675)
XLA Ops:
  7.2 2.3 fusion.137
  9.5 0.0 all-gather.21.cloned.1.call-start
  9.6 2.3 fusion.136
  11.9 0.7 all-gather.19.cloned.1.call-update
  12.6 0.5 all-gather.17.cloned.1.call-update
  13.2 49.1 %all-gather.23.cloned.1.call-done = bf16[1,4096,1024]{2,1,0:T(8,128)(2,1)} async-done(((bf16[1,256,1024]{2,1,0:T(8,128)(2,1)}), bf16[1,4096,1024]{2,1,0:T(8,128)(2,1)}) %all-gather.23.cloned.1.call-update) | async-done | bytes 8388624 | tf_op jit(solution)/shard_map/all_gather | solution.py:56
  62.3 3.1 constant_dynamic-slice_fusion.3
  65.4 0.0 all-gather.27.cloned.1.call-start
  65.5 48.3 %all-gather.21.cloned.1.call-done = bf16[1,1024,4096]{2,1,0:T(8,128)(2,1)} async-done(((bf16[1,64,4096]{2,1,0:T(8,128)(2,1)}), bf16[1,1024,4096]{2,1,0:T(8,128)(2,1)}) %all-gather.21.cloned.1.call-update) | async-done | bytes 8388624 | tf_op jit(solution)/shard_map/all_gather | solution.py:55
  113.8 3.1 constant_dynamic-slice_fusion.2
  117.0 6.0 fusion.135
  123.0 6.5 copy.22
  129.6 6.5 copy.23
  136.1 3.1 fusion.58
  139.1 0.6 copy-done.14
  139.7 3.1 fusion.62
  142.8 0.6 copy-done.16
  143.4 21.3 %all-gather.19.cloned.1.call-done = bf16[1,4096,1024]{2,1,0:T(8,128)(2,1)} async-done(((bf16[1,256,1024]{2,1,0:T(8,128)(2,1)}), bf16[1,4096,1024]{2,1,0:T(8,128)(2,1)}) %all-gather.19.cloned.1.call-update) | async-done | bytes 8388624 | tf_op jit(solution)/shard_map/all_gather | solution.py:56
  164.7 3.1 constant_dynamic-slice_fusion.1
  167.8 0.3 all-gather.31.cloned.1.call-start
  168.2 47.3 %all-gather.17.cloned.1.call-done = bf16[1,1024,4096]{2,1,0:T(8,128)(2,1)} async-done(((bf16[1,64,4096]{2,1,0:T(8,128)(2,1)}), bf16[1,1024,4096]{2,1,0:T(8,128)(2,1)}) %all-gather.17.cloned.1.call-update) | async-done | bytes 8388624 | tf_op jit(solution)/shard_map/all_gather | solution.py:55
  215.5 25.2 %convolution_convert_fusion.1 = bf16[2048,4096]{1,0:T(8,128)(2,1)} fusion(bf16[1,1024,4096]{2,1,0:T(8,128)(2,1)} %all-gather.17.cloned.1.call-done, bf16[1,2048,1024]{1,2,0:T(8,128)(2,1)} %copy.23, f32[2048]{0:T(1024)S(1)} %fusion.119), kind=kOutput, calls=%fused_computation.85 | convolution fusion | flops 17194549248 | bytes 29368320 | tf_op jit(solution)/shard_map/dot_general | solution.py:21
  240.7 26.3 %fusion.54 = (f32[2048]{0:T(1024)S(1)}, bf16[2048,1024]{0,1:T(8,128)(2,1)}) fusion(bf16[1,4096,1024]{2,1,0:T(8,128)(2,1)} %all-gather.19.cloned.1.call-done, bf16[2048,4096]{1,0:T(8,128)(2,1)} %convolution_convert_fusion.1, bf16[1,2048,1024]{1,2,0:T(8,128)(2,1)} %copy.23), kind=kOutput, calls=%fused_computation.108 | convolution fusion | flops 17276336128 | bytes 33562624 | tf_op jit(solution)/shard_map/dot_general | solution.py:23
  267.0 0.6 copy-done.30
  267.6 23.8 %convolution_convert_fusion.3 = bf16[2048,4096]{1,0:T(8,128)(2,1)} fusion(bf16[1,1024,4096]{2,1,0:T(8,128)(2,1)} %all-gather.17.cloned.1.call-done, bf16[1,2048,1024]{1,2,0:T(8,128)(2,1)S(1)} %copy-done, f32[2048]{0:T(1024)S(1)} %fusion.117), kind=kOutput, calls=%fused_computation.87 | convolution fusion | flops 17194549248 | bytes 29368320 | tf_op jit(solution)/shard_map/dot_general | solution.py:21
  291.4 25.4 %fusion.50 = (f32[2048]{0:T(1024)S(1)}, bf16[2048,1024]{0,1:T(8,128)(2,1)}) fusion(bf16[1,4096,1024]{2,1,0:T(8,128)(2,1)} %all-gather.19.cloned.1.call-done, bf16[2048,4096]{1,0:T(8,128)(2,1)} %convolution_convert_fusion.3, bf16[1,2048,1024]{1,2,0:T(8,128)(2,1)S(1)} %copy-done), kind=kOutput, calls=%fused_computation.104 | convolution fusion | flops 17276336128 | bytes 33562624 | tf_op jit(solution)/shard_map/dot_general | solution.py:23
  316.9 0.6 copy-done.28
  317.5 3.2 constant_dynamic-slice_fusion
  320.8 25.5 %convolution_convert_fusion.2 = bf16[2048,4096]{1,0:T(8,128)(2,1)} fusion(bf16[1,1024,4096]{2,1,0:T(8,128)(2,1)} %all-gather.21.cloned.1.call-done, bf16[2048,1024]{0,1:T(8,128)(2,1)} %get-tuple-element.19, f32[2048]{0:T(1024)S(1)} %fusion.118), kind=kOutput, calls=%fused_computation.86 | convolution fusion | flops 17194549248 | bytes 29368320 | tf_op jit(solution)/shard_map/dot_general | solution.py:21
  346.3 24.1 %convolution_convert_fusion = bf16[2048,4096]{1,0:T(8,128)(2,1)} fusion(bf16[1,1024,4096]{2,1,0:T(8,128)(2,1)} %all-gather.21.cloned.1.call-done, bf16[2048,1024]{0,1:T(8,128)(2,1)S(1)} %copy-done.10, f32[2048]{0:T(1024)S(1)} %fusion.120), kind=kOutput, calls=%fused_computation.84 | convolution fusion | flops 17194549248 | bytes 29368320 | tf_op jit(solution)/shard_map/dot_general | solution.py:21
  370.4 28.9 %fusion.96 = f32[4096,1024]{1,0:T(8,128)} fusion(bf16[2,2048,1024]{2,1,0:T(8,128)(2,1)} %param.5, bf16[2048,4096]{1,0:T(8,128)(2,1)} %convolution_convert_fusion.2), kind=kOutput, calls=%fused_computation.152 | convolution fusion | flops 17263755264 | bytes 37748736 | tf_op jit(solution)/shard_map/tf,tm->fm/dot_general | solution.py:35
  399.3 34.2 %convolution_add_fusion.2 = f32[4096,1024]{1,0:T(8,128)} fusion(f32[4096,1024]{1,0:T(8,128)} %fusion.96, bf16[2,2048,1024]{2,1,0:T(8,128)(2,1)} %param.5, bf16[2048,4096]{1,0:T(8,128)(2,1)} %convolution_convert_fusion), kind=kOutput, calls=%fused_computation.94 | convolution fusion | flops 17267949568 | bytes 54525952 | tf_op jit(solution)/shard_map/tf,tm->fm/dot_general | solution.py:35
  433.6 6.3 fusion.134
  439.9 6.6 copy.24
  446.4 6.6 copy.25
  453.0 44.2 %fusion.6 = bf16[2048,4096]{1,0:T(8,128)(2,1)} fusion(bf16[2048,4096]{1,0:T(8,128)(2,1)} %convolution_convert_fusion, bf16[1,4096,1024]{2,1,0:T(8,128)(2,1)} %all-gather.25.cloned.1.call-done, bf16[2,2048,1024]{2,1,0:T(8,128)(2,1)} %param.5), kind=kOutput, calls=%fused_computation.26 | convolution fusion | flops 17356029952 | bytes 46137344 | tf_op jit(solution)/shard_map/tm,fm->tf/dot_general | solution.py:28
  497.2 23.4 %fusion.57 = (f32[2048]{0:T(1024)S(1)}, f32[2048,1024]{0,1:T(8,128)S(1)}) fusion(bf16[2048,1024]{0,1:T(8,128)(2,1)} %get-tuple-element.17, bf16[2048,4096]{1,0:T(8,128)(2,1)} %fusion.6, bf16[1,1024,4096]{2,1,0:T(8,128)(2,1)} %all-gather.27.cloned.1.call-done), kind=kOutput, calls=%fused_computation.111 | convolution fusion | flops 17186158592 | bytes 37756928 | tf_op jit(solution)/shard_map/tf,mf->tm/dot_general | solution.py:31
  520.6 44.3 %fusion.12 = bf16[2048,4096]{1,0:T(8,128)(2,1)} fusion(bf16[2048,4096]{1,0:T(8,128)(2,1)} %convolution_convert_fusion.2, bf16[1,4096,1024]{2,1,0:T(8,128)(2,1)} %all-gather.25.cloned.1.call-done, bf16[2,2048,1024]{2,1,0:T(8,128)(2,1)} %param.5), kind=kOutput, calls=%fused_computation.32 | convolution fusion | flops 17356029952 | bytes 46137344 | tf_op jit(solution)/shard_map/tm,fm->tf/dot_general | solution.py:28
  565.0 24.6 %fusion.53 = (f32[2048]{0:T(1024)S(1)}, f32[2048,1024]{0,1:T(8,128)}) fusion(bf16[2048,1024]{0,1:T(8,128)(2,1)S(1)} %copy-done.13, bf16[2048,4096]{1,0:T(8,128)(2,1)} %fusion.12, bf16[1,1024,4096]{2,1,0:T(8,128)(2,1)} %all-gather.27.cloned.1.call-done), kind=kOutput, calls=%fused_computation.107 | convolution fusion | flops 17186158592 | bytes 37756928 | tf_op jit(solution)/shard_map/tf,mf->tm/dot_general | solution.py:31
  589.6 4.3 fusion.47
  593.9 4.8 fusion.43
  598.7 2.0 copy-done.6
  600.7 28.2 %fusion.131 = f32[4096,1024]{1,0:T(8,128)} fusion(bf16[2048,1024]{0,1:T(8,128)(2,1)S(1)} %fusion.43, bf16[2048,4096]{1,0:T(8,128)(2,1)} %convolution_convert_fusion.3), kind=kOutput, calls=%fused_computation.179 | convolution fusion | flops 17263755264 | bytes 37748736 | tf_op jit(solution)/shard_map/tf,tm->fm/dot_general | solution.py:35
  628.9 34.7 %convolution_add_fusion.3 = f32[4096,1024]{1,0:T(8,128)} fusion(f32[4096,1024]{1,0:T(8,128)} %fusion.131, bf16[2048,1024]{0,1:T(8,128)(2,1)} %fusion.47, bf16[2048,4096]{1,0:T(8,128)(2,1)} %convolution_convert_fusion.1), kind=kOutput, calls=%fused_computation.95 | convolution fusion | flops 17267949568 | bytes 54525952 | tf_op jit(solution)/shard_map/tf,tm->fm/dot_general | solution.py:35
  663.7 23.6 %fusion.114 = f32[1024,4096]{1,0:T(8,128)} fusion(bf16[2048,4096]{1,0:T(8,128)(2,1)} %fusion.12, bf16[2048,1024]{0,1:T(8,128)(2,1)} %get-tuple-element.19, f32[2048]{0:T(1024)S(1)} %copy-done.27), kind=kOutput, calls=%fused_computation.156 | convolution fusion | flops 17186160640 | bytes 37756928 | tf_op jit(solution)/shard_map/tm,tf->mf/dot_general | solution.py:34
  687.3 27.9 %convolution_add_fusion = f32[1024,4096]{1,0:T(8,128)} fusion(f32[1024,4096]{1,0:T(8,128)} %fusion.114, bf16[2048,4096]{1,0:T(8,128)(2,1)} %fusion.6, bf16[2048,1024]{0,1:T(8,128)(2,1)} %get-tuple-element.17, f32[2048]{0:T(1024)S(1)} %copy-done.25), kind=kOutput, calls=%fused_computation.92 | convolution fusion | flops 17190354944 | bytes 54534144 | tf_op jit(solution)/shard_map/tm,tf->mf/dot_general | solution.py:34
  715.3 49.0 %fusion.15 = bf16[2048,4096]{1,0:T(8,128)(2,1)} fusion(bf16[2048,4096]{1,0:T(8,128)(2,1)} %convolution_convert_fusion.3, bf16[2048,1024]{0,1:T(8,128)(2,1)} %copy-done.6, bf16[1,4096,1024]{2,1,0:T(8,128)(2,1)} %all-gather.29.cloned.1.call-done), kind=kOutput, calls=%fused_computation.35 | convolution fusion | flops 17356029952 | bytes 46137344 | tf_op jit(solution)/shard_map/tm,fm->tf/dot_general | solution.py:28
  764.3 22.4 %fusion.109 = f32[1024,4096]{1,0:T(8,128)} fusion(bf16[2048,4096]{1,0:T(8,128)(2,1)} %fusion.15, bf16[1,2048,1024]{1,2,0:T(8,128)(2,1)S(1)} %copy-done.1, f32[2048]{0:T(1024)S(1)} %copy-done.19), kind=kOutput, calls=%fused_computation.155 | convolution fusion | flops 17186160640 | bytes 37756928 | tf_op jit(solution)/shard_map/tm,tf->mf/dot_general | solution.py:34
  786.7 47.5 %fusion.9 = bf16[2048,4096]{1,0:T(8,128)(2,1)} fusion(bf16[2048,4096]{1,0:T(8,128)(2,1)} %convolution_convert_fusion.1, bf16[2048,1024]{0,1:T(8,128)(2,1)S(1)} %copy-done.8, bf16[1,4096,1024]{2,1,0:T(8,128)(2,1)} %all-gather.29.cloned.1.call-done), kind=kOutput, calls=%fused_computation.29 | convolution fusion | flops 17356029952 | bytes 46137344 | tf_op jit(solution)/shard_map/tm,fm->tf/dot_general | solution.py:28
  834.3 28.1 %convolution_add_fusion.1 = f32[1024,4096]{1,0:T(8,128)} fusion(f32[1024,4096]{1,0:T(8,128)} %fusion.109, bf16[2048,4096]{1,0:T(8,128)(2,1)} %fusion.9, bf16[1,2048,1024]{1,2,0:T(8,128)(2,1)} %copy.23, f32[2048]{0:T(1024)S(1)} %copy-done.22), kind=kOutput, calls=%fused_computation.93 | convolution fusion | flops 17190354944 | bytes 54534144 | tf_op jit(solution)/shard_map/tm,tf->mf/dot_general | solution.py:34
  862.4 25.3 %fusion.91 = bf16[1,2048,1024]{1,2,0:T(8,128)(2,1)} fusion(bf16[2048,1024]{0,1:T(8,128)(2,1)} %get-tuple-element.19, bf16[1,4096,1024]{2,1,0:T(8,128)(2,1)} %all-gather.23.cloned.1.call-done, bf16[2048,4096]{1,0:T(8,128)(2,1)} %convolution_convert_fusion.2), kind=kOutput, calls=%fused_computation.147 | convolution fusion | flops 17270046720 | bytes 33554432 | tf_op jit(solution)/shard_map/dot_general | solution.py:23
  887.8 25.2 %fusion.90 = bf16[1,2048,1024]{1,2,0:T(8,128)(2,1)} fusion(bf16[2048,1024]{0,1:T(8,128)(2,1)S(1)} %copy-done.12, bf16[1,4096,1024]{2,1,0:T(8,128)(2,1)} %all-gather.23.cloned.1.call-done, bf16[2048,4096]{1,0:T(8,128)(2,1)} %convolution_convert_fusion), kind=kOutput, calls=%fused_computation.146 | convolution fusion | flops 17270046720 | bytes 33554432 | tf_op jit(solution)/shard_map/dot_general | solution.py:23
  913.0 7.6 pad_maximum_fusion
  920.6 11.8 copy.16
  932.5 24.6 %fusion.65 = (f32[2048]{0:T(1024)S(1)}, f32[2048,1024]{0,1:T(8,128)}) fusion(bf16[1,2048,1024]{1,2,0:T(8,128)(2,1)} %copy.23, bf16[2048,4096]{1,0:T(8,128)(2,1)} %fusion.9, bf16[1,1024,4096]{2,1,0:T(8,128)(2,1)} %all-gather.31.cloned.1.call-done), kind=kOutput, calls=%fused_computation.119 | convolution fusion | flops 17186158592 | bytes 37756928 | tf_op jit(solution)/shard_map/tf,mf->tm/dot_general | solution.py:31
  957.2 22.3 %fusion.61 = (f32[2048]{0:T(1024)S(1)}, f32[2048,1024]{0,1:T(8,128)}) fusion(bf16[1,2048,1024]{1,2,0:T(8,128)(2,1)S(1)} %copy-done.2, bf16[2048,4096]{1,0:T(8,128)(2,1)} %fusion.15, bf16[1,1024,4096]{2,1,0:T(8,128)(2,1)S(1)} %copy-done.32), kind=kOutput, calls=%fused_computation.115 | convolution fusion | flops 17186158592 | bytes 37756928 | tf_op jit(solution)/shard_map/tf,mf->tm/dot_general | solution.py:31
  979.5 5.2 fusion.92
  984.7 6.3 fusion.93
  991.0 6.2 pad_maximum_fusion.1
  997.3 11.8 copy.17
  1009.1 3.1 pad_maximum_fusion.3
  1012.2 81.0 %reduce-scatter.7.cloned.1.call-done = f32[64,4096]{1,0:T(8,128)} async-done(((f32[1024,4096]{1,0:T(8,128)}), f32[64,4096]{1,0:T(8,128)}) %reduce-scatter.7.cloned.1.call-update) | async-done | bytes 1048592 | tf_op jit(solution)/shard_map/reduce_scatter | solution.py:72
  1093.3 177.7 %reduce-scatter.5.cloned.1.call-done = f32[64,4096]{1,0:T(8,128)} async-done(((f32[1024,4096]{1,0:T(8,128)}), f32[64,4096]{1,0:T(8,128)}) %reduce-scatter.5.cloned.1.call-update) | async-done | bytes 1048592 | tf_op jit(solution)/shard_map/reduce_scatter | solution.py:72
  1270.9 3.1 pad_maximum_fusion.2
  (94 shorter events, 0.8 us)
Async XLA Ops:
  7.2 55.1 %all-gather.23.cloned.1.call-start = ((), (), s32[]{:S(2)}) async-start(), calls=%async_computation.11 | async-start | bytes 8912896 | tf_op jit(solution)/shard_map/all_gather | solution.py:56
  9.5 104.3 %all-gather.21.cloned.1.call-start = ((), (), s32[]{:S(2)}) async-start(), calls=%async_computation.10 | async-start | bytes 8912896 | tf_op jit(solution)/shard_map/all_gather | solution.py:55
  11.9 152.9 %all-gather.19.cloned.1.call-start = ((), (), s32[]{:S(2)}) async-start(), calls=%async_computation.9 | async-start | bytes 8912896 | tf_op jit(solution)/shard_map/all_gather | solution.py:56
  12.6 202.9 %all-gather.17.cloned.1.call-start = ((), (), s32[]{:S(2)}) async-start(), calls=%async_computation.8 | async-start | bytes 8912896 | tf_op jit(solution)/shard_map/all_gather | solution.py:55
  13.2 439.8 %all-gather.25.cloned.1.call-start = ((), (), s32[]{:S(2)}) async-start(), calls=%async_computation.12 | async-start | bytes 10485760 | tf_op jit(solution)/shard_map/all_gather | solution.py:67
  65.4 431.8 %all-gather.27.cloned.1.call-start = ((), (), s32[]{:S(2)}) async-start(), calls=%async_computation.13 | async-start | bytes 10485760 | tf_op jit(solution)/shard_map/all_gather | solution.py:66
  116.9 598.4 %all-gather.29.cloned.1.call-start = ((), (), s32[]{:S(2)}) async-start(), calls=%async_computation.14 | async-start | bytes 10485760 | tf_op jit(solution)/shard_map/all_gather | solution.py:67
  139.1 0.6 copy-start.14
  139.7 127.9 %copy-start.18 = (f32[2048]{0:T(1024)}, f32[2048]{0:T(1024)S(1)}, u32[]{:S(2)}) copy-start(f32[2048]{0:T(1024)S(1)} %fusion.117) | copy-start | bytes 24580
  142.8 0.6 copy-start.16
  143.4 72.1 %copy-start.21 = (f32[2048]{0:T(1024)}, f32[2048]{0:T(1024)S(1)}, u32[]{:S(2)}) copy-start(f32[2048]{0:T(1024)S(1)} %fusion.119) | copy-start | bytes 24580
  167.8 764.6 %all-gather.31.cloned.1.call-start = ((), (), s32[]{:S(2)}) async-start(), calls=%async_computation.15 | async-start | bytes 10485760 | tf_op jit(solution)/shard_map/all_gather | solution.py:66
  240.7 26.9 %copy-start = (bf16[1,2048,1024]{1,2,0:T(8,128)(2,1)S(1)}, bf16[1,2048,1024]{1,2,0:T(8,128)(2,1)}, u32[]{:S(2)}) copy-start(bf16[1,2048,1024]{1,2,0:T(8,128)(2,1)} %copy.22) | copy-start | bytes 12582916
  267.0 0.6 copy-start.30
  267.6 78.7 %copy-start.24 = (f32[2048]{0:T(1024)}, f32[2048]{0:T(1024)S(1)}, u32[]{:S(2)}) copy-start(f32[2048]{0:T(1024)S(1)} %fusion.120) | copy-start | bytes 24580
  316.9 0.6 copy-start.28
  317.5 28.8 %copy-start.26 = (f32[2048]{0:T(1024)}, f32[2048]{0:T(1024)S(1)}, u32[]{:S(2)}) copy-start(f32[2048]{0:T(1024)S(1)} %fusion.118) | copy-start | bytes 24580
  320.7 688.4 %reduce-scatter.11.cloned.1.call-start = ((), (), s32[]{:S(2)}) async-start(), calls=%async_computation.7 | async-start | bytes 17825792 | tf_op jit(solution)/shard_map/reduce_scatter | solution.py:73
  320.8 25.6 %copy-start.10 = (bf16[2048,1024]{0,1:T(8,128)(2,1)S(1)}, bf16[2048,1024]{0,1:T(8,128)(2,1)}, u32[]{:S(2)}) copy-start(bf16[2048,1024]{0,1:T(8,128)(2,1)} %get-tuple-element.17) | copy-start | bytes 12582916
  433.6 575.6 %reduce-scatter.9.cloned.1.call-start = ((), (), s32[]{:S(2)}) async-start(), calls=%async_computation.6 | async-start | bytes 17825792 | tf_op jit(solution)/shard_map/reduce_scatter | solution.py:73
  497.2 23.4 %copy-start.31 = (f32[2048]{0:T(1024)S(1)}, f32[2048]{0:T(1024)}, u32[]{:S(2)}) copy-start(f32[2048]{0:T(1024)} %copy-done.30) | copy-start | bytes 24580
  520.6 44.3 %copy-start.13 = (bf16[2048,1024]{0,1:T(8,128)(2,1)S(1)}, bf16[2048,1024]{0,1:T(8,128)(2,1)}, u32[]{:S(2)}) copy-start(bf16[2048,1024]{0,1:T(8,128)(2,1)} %get-tuple-element.19) | copy-start | bytes 12582916
  564.9 24.6 %copy-start.29 = (f32[2048]{0:T(1024)S(1)}, f32[2048]{0:T(1024)}, u32[]{:S(2)}) copy-start(f32[2048]{0:T(1024)} %copy-done.28) | copy-start | bytes 24580
  564.9 24.6 %copy-start.5 = (bf16[1,2048,1024]{1,2,0:T(8,128)(2,1)S(1)}, bf16[1,2048,1024]{1,2,0:T(8,128)(2,1)}, u32[]{:S(2)}) copy-start(bf16[1,2048,1024]{1,2,0:T(8,128)(2,1)} %copy.25) | copy-start | bytes 12582916
  564.9 24.6 %copy-start.11 = (bf16[2048,1024]{0,1:T(8,128)(2,1)S(1)}, bf16[2048,1024]{0,1:T(8,128)(2,1)}, u32[]{:S(2)}) copy-start(bf16[2048,1024]{0,1:T(8,128)(2,1)} %get-tuple-element.17) | copy-start | bytes 12582916
  565.0 24.6 %copy-start.25 = (f32[2048]{0:T(1024)S(1)}, f32[2048]{0:T(1024)}, u32[]{:S(2)}) copy-start(f32[2048]{0:T(1024)} %copy-done.24) | copy-start | bytes 24580
  589.5 4.4 copy-start.4
  589.5 4.4 copy-start.27
  598.7 2.0 copy-start.6
  663.7 429.6 %reduce-scatter.7.cloned.1.call-start = ((), (), s32[]{:S(2)}) async-start(), calls=%async_computation.5 | async-start | bytes 17825792 | tf_op jit(solution)/shard_map/reduce_scatter | solution.py:72
  715.2 49.1 %copy-start.19 = (f32[2048]{0:T(1024)S(1)}, f32[2048]{0:T(1024)}, u32[]{:S(2)}) copy-start(f32[2048]{0:T(1024)} %copy-done.18) | copy-start | bytes 24580
  715.2 555.7 %reduce-scatter.5.cloned.1.call-start = ((), (), s32[]{:S(2)}) async-start(), calls=%async_computation.4 | async-start | bytes 17825792 | tf_op jit(solution)/shard_map/reduce_scatter | solution.py:72
  715.3 49.0 %copy-start.1 = (bf16[1,2048,1024]{1,2,0:T(8,128)(2,1)S(1)}, bf16[1,2048,1024]{1,2,0:T(8,128)(2,1)}, u32[]{:S(2)}) copy-start(bf16[1,2048,1024]{1,2,0:T(8,128)(2,1)} %copy.22) | copy-start | bytes 12582916
  764.3 22.4 %copy-start.8 = (bf16[2048,1024]{0,1:T(8,128)(2,1)S(1)}, bf16[2048,1024]{0,1:T(8,128)(2,1)}, u32[]{:S(2)}) copy-start(bf16[2048,1024]{0,1:T(8,128)(2,1)} %fusion.47) | copy-start | bytes 12582916
  786.7 47.5 %copy-start.22 = (f32[2048]{0:T(1024)S(1)}, f32[2048]{0:T(1024)}, u32[]{:S(2)}) copy-start(f32[2048]{0:T(1024)} %copy-done.21) | copy-start | bytes 24580
  862.4 25.3 %copy-start.12 = (bf16[2048,1024]{0,1:T(8,128)(2,1)S(1)}, bf16[2048,1024]{0,1:T(8,128)(2,1)}, u32[]{:S(2)}) copy-start(bf16[2048,1024]{0,1:T(8,128)(2,1)} %get-tuple-element.17) | copy-start | bytes 12582916
  932.5 24.6 %copy-start.17 = (f32[2048]{0:T(1024)S(1)}, f32[2048]{0:T(1024)}, u32[]{:S(2)}) copy-start(f32[2048]{0:T(1024)} %copy-done.16) | copy-start | bytes 24580
  932.5 24.6 %copy-start.2 = (bf16[1,2048,1024]{1,2,0:T(8,128)(2,1)S(1)}, bf16[1,2048,1024]{1,2,0:T(8,128)(2,1)}, u32[]{:S(2)}) copy-start(bf16[1,2048,1024]{1,2,0:T(8,128)(2,1)} %copy.22) | copy-start | bytes 12582916
  932.5 24.6 %copy-start.32 = (bf16[1,1024,4096]{2,1,0:T(8,128)(2,1)S(1)}, bf16[1,1024,4096]{2,1,0:T(8,128)(2,1)}, u32[]{:S(2)}) copy-start(bf16[1,1024,4096]{2,1,0:T(8,128)(2,1)} %all-gather.31.cloned.1.call-done) | copy-start | bytes 25165828
  957.1 22.3 %copy-start.15 = (f32[2048]{0:T(1024)S(1)}, f32[2048]{0:T(1024)}, u32[]{:S(2)}) copy-start(f32[2048]{0:T(1024)} %copy-done.14) | copy-start | bytes 24580
  957.1 22.3 %copy-start.3 = (bf16[1,2048,1024]{1,2,0:T(8,128)(2,1)S(1)}, bf16[1,2048,1024]{1,2,0:T(8,128)(2,1)}, u32[]{:S(2)}) copy-start(bf16[1,2048,1024]{1,2,0:T(8,128)(2,1)} %copy.23) | copy-start | bytes 12582916
  957.1 22.3 %copy-start.9 = (bf16[2048,1024]{0,1:T(8,128)(2,1)S(1)}, bf16[2048,1024]{0,1:T(8,128)(2,1)}, u32[]{:S(2)}) copy-start(bf16[2048,1024]{0,1:T(8,128)(2,1)} %fusion.47) | copy-start | bytes 12582916
  957.1 22.3 %copy-start.23 = (f32[2048]{0:T(1024)S(1)}, f32[2048]{0:T(1024)}, u32[]{:S(2)}) copy-start(f32[2048]{0:T(1024)} %copy-done.21) | copy-start | bytes 24580
  979.4 5.3 copy-start.7
  979.4 5.3 copy-start.20
Sparse Core Ops, SparseCore 0:
  10.8 51.4 all-gather.22
  65.1 48.6 all-gather.20
  116.0 48.6 all-gather.18
  166.8 48.6 all-gather.16
  217.7 83.6 all-gather.24
  303.6 83.6 all-gather.26
  389.1 83.6 all-gather.28
  474.5 83.6 all-gather.30
  560.5 177.2 reduce-scatter.10
  739.9 175.4 reduce-scatter.8
  917.7 175.4 reduce-scatter.6
  1095.4 175.4 reduce-scatter.4
where the time goes:
time: 1290 us; the launch traced here: 1280 us
  matrix products  709 us (55%)
  waiting for transfers between devices  426 us (33%)
  local copies, waits for them, and re-layouts  83.6 us (6%)
  other arithmetic  46.9 us (4%)
  between operations  14.7 us (1%)
    reduce_scatter x4, waiting for transfers between devices, body(): lax.psum_scatter(total, ALL_AXES, scatter_dimension=0, tiled=True)  259 us
    dot_general x4, matrix products, layer_backward(): jnp.einsum('tm,fm->tf', d_out, down_mat, preferred_element_type=jnp.float32)  185 us
    dot_general x4, matrix products, layer_backward(): jnp.einsum('tf,tm->fm', hidden, d_out, preferred_element_type=jnp.float32)  126 us
    dot_general x4, matrix products, layer_forward(): jnp.dot(hidden, down_mat, preferred_element_type=jnp.float32)  102 us
    dot_general x4, matrix products, layer_backward(): jnp.einsum('tm,tf->mf', normed, d_pre, preferred_element_type=jnp.float32)  102 us
    dot_general x4, matrix products, layer_forward(): jnp.dot(normed, up_mat, preferred_element_type=jnp.float32)  98.6 us
    all_gather x2, waiting for transfers between devices, body(): full_up = lax.all_gather(w_up[layer_idx], ALL_AXES, axis=0, tiled=True)  95.6 us
    dot_general x4, matrix products, layer_backward(): jnp.einsum('tf,mf->tm', d_pre, up_mat, preferred_element_type=jnp.float32)  94.9 us
  transfers between devices with their start and end apart: 12, of which 6 were waited for; matrix products, arithmetic and copies ran while one was open for 65% of the time, Pallas kernels for 0%

commit v1 on v0

v1 whole, which is shorter than its diff:
```python
import functools

import jax
import jax.numpy as jnp
from jax import lax
from jax.experimental import pallas as pl
from jax.experimental.pallas import tpu as pltpu
from jax.sharding import PartitionSpec as P


NORM_EPS = 1e-6
ALL_AXES = ("local", "data")
GELU_A = 0.7978845608028654
GELU_B = GELU_A * 0.044715

RING = (0, 1, 3, 2, 6, 7, 5, 4)
TWIN = (2, 5, 0, 7, 6, 1, 4, 3)
RING_POS = tuple(RING.index(chip) for chip in range(8))
GROUP = [[2 * chip + core for chip in RING for core in (0, 1)]]
TO_TWIN = [(2 * chip + core, 2 * TWIN[chip] + core) for chip in range(8) for core in (0, 1)]
TO_PARTNER = [(dev, dev ^ 1) for dev in range(16)]
VMEM_LIMIT = 60 * 1024 * 1024


def params(semantics=("arbitrary",)):
    return pltpu.CompilerParams(dimension_semantics=semantics, vmem_limit_bytes=VMEM_LIMIT)


def cost(tokens, hidden, ffn, moved, transcendentals=0):
    return pl.CostEstimate(flops=2 * tokens * hidden * ffn, bytes_accessed=moved, transcendentals=transcendentals)


def dot(a, b, a_dim=1, b_dim=0):
    return lax.dot_general(a, b, (((a_dim,), (b_dim,)), ((), ())), preferred_element_type=jnp.float32)


def gate_of(a):
    sq = a * a
    return 0.5 + 0.5 * jnp.tanh(a * (GELU_A + GELU_B * sq)), sq


def lane_tiles(value, source):
    width = value.shape[-1] // len(source)
    return jnp.concatenate([value[:, k * width:(k + 1) * width] for k in source], axis=-1)


def up_kernel(q_ref, in_ref, w_ref, *refs, normalize, chunk, first):
    a_ref, s_ref, kept_ref = refs[-3:]
    if normalize:
        u_ref = refs[-4]
        x = in_ref[...].astype(jnp.float32)
        u = (x * lax.rsqrt(jnp.mean(x * x, axis=-1, keepdims=True) + NORM_EPS)).astype(jnp.bfloat16)
        u_ref[...] = lane_tiles(u, RING)
    else:
        u_ref = in_ref
    blocks = w_ref.shape[1] // chunk
    for n in range(blocks):
        cols = pl.ds((RING_POS[first + n] % blocks) * chunk, chunk)
        a = dot(u_ref[...], w_ref[:, n * chunk:(n + 1) * chunk]).astype(jnp.bfloat16)
        a_ref[:, cols] = a
        a = a.astype(jnp.float32)
        s_ref[:, cols] = (a * gate_of(a)[0]).astype(jnp.bfloat16)

    @pl.when(pl.program_id(0) == 0)
    def _():
        rows = kept_ref.shape[0]
        kept_ref[...] = w_ref[pl.ds(pl.multiple_of(q_ref[0] * rows, rows), rows), :]


def up_call(quarter, source, w, ffn, half=0, prior=None, tile=512):
    tokens, hidden = source.shape
    width = w.shape[1]
    row = lambda i, q: (i, 0)
    column = lambda i, q: (i, half)
    fresh = prior is None
    wide = jax.ShapeDtypeStruct((tokens, ffn), jnp.bfloat16)
    out_specs = [pl.BlockSpec((tile, width), column)] * 2 + [pl.BlockSpec((hidden // 4, width), lambda i, q: (0, half))]
    out_shape = [wide, wide, jax.ShapeDtypeStruct((hidden // 4, ffn), jnp.bfloat16)]
    in_specs = [pl.BlockSpec((tile, hidden), row), pl.BlockSpec((hidden, width), lambda i, q: (0, 0))]
    if fresh:
        out_specs = [pl.BlockSpec((tile, hidden), row)] + out_specs
        out_shape = [jax.ShapeDtypeStruct((tokens, hidden), jnp.bfloat16)] + out_shape
    else:
        in_specs = in_specs + [pl.BlockSpec(memory_space=pl.ANY)] * 3
    return pl.pallas_call(
        functools.partial(up_kernel, normalize=fresh, chunk=ffn // 8, first=8 * half * width // ffn),
        grid_spec=pltpu.PrefetchScalarGridSpec(
            num_scalar_prefetch=1, grid=(tokens // tile,), in_specs=in_specs, out_specs=out_specs
        ),
        out_shape=out_shape,
        input_output_aliases={} if fresh else {3: 0, 4: 1, 5: 2},
        compiler_params=params(),
        cost_estimate=cost(tokens, hidden, width, 4 * tokens * (hidden + width) + 2 * hidden * width, tokens * width),
        name="up",
    )(quarter, source, w, *(prior or ()))


def down_kernel(q_ref, s_ref, x_ref, w_ref, o_ref, kept_ref, *, chunk):
    for n in range(w_ref.shape[1] // chunk):
        cols = pl.ds(n * chunk, chunk)
        o_ref[:, cols] = (x_ref[:, cols].astype(jnp.float32) + dot(s_ref[...], w_ref[:, cols])).astype(jnp.bfloat16)

    @pl.when(pl.program_id(0) == 0)
    def _():
        rows = kept_ref.shape[0]
        kept_ref[...] = w_ref[pl.ds(pl.multiple_of(q_ref[0] * rows, rows), rows), :]


def down_call(quarter, s, x, w, tile=512, chunk=512):
    tokens, hidden = x.shape
    ffn = s.shape[1]
    row = lambda i, q: (i, 0)
    whole = lambda i, q: (0, 0)
    return pl.pallas_call(
        functools.partial(down_kernel, chunk=chunk),
        grid_spec=pltpu.PrefetchScalarGridSpec(
            num_scalar_prefetch=1,
            grid=(tokens // tile,),
            in_specs=[pl.BlockSpec((tile, ffn), row), pl.BlockSpec((tile, hidden), row), pl.BlockSpec((ffn, hidden), whole)],
            out_specs=[pl.BlockSpec((tile, hidden), row), pl.BlockSpec((ffn // 4, hidden), whole)],
        ),
        out_shape=[
            jax.ShapeDtypeStruct((tokens, hidden), jnp.bfloat16),
            jax.ShapeDtypeStruct((ffn // 4, hidden), jnp.bfloat16),
        ],
        compiler_params=params(),
        cost_estimate=cost(tokens, hidden, ffn, 2 * tokens * (2 * hidden + ffn) + 2 * hidden * ffn),
        name="down",
    )(quarter, s, x, w)


def weight_grad_kernel(l_ref, r_ref, o_ref, *, chunk):
    for n in range(r_ref.shape[1] // chunk):
        cols = pl.ds(n * chunk, chunk)
        o_ref[:, cols] = dot(l_ref[...], r_ref[:, cols], 0, 0)


def weight_grad_call(left, right, rows, columns, chunk):
    tokens, m = left.shape
    n = right.shape[1]
    return pl.pallas_call(
        functools.partial(weight_grad_kernel, chunk=chunk),
        grid=(m // rows, n // columns),
        in_specs=[pl.BlockSpec((tokens, rows), lambda i, j: (0, i)), pl.BlockSpec((tokens, columns), lambda i, j: (0, j))],
        out_specs=pl.BlockSpec((rows, columns), lambda i, j: (i, j)),
        out_shape=jax.ShapeDtypeStruct((m, n), jnp.float32),
        compiler_params=params(("arbitrary", "arbitrary")),
        cost_estimate=cost(tokens, m, n, 2 * tokens * (m + n) + 4 * m * n),
    )(left, right)


def act_grad_kernel(q_ref, c_ref, a_ref, w0, w1, *refs, first):
    z_ref = refs[-1]
    for rel, w_ref in enumerate((w0, w1)):
        held = q_ref[0] ^ (first + rel)
        chunk = w_ref.shape[0] // 2
        for n in range(2):
            spot = 2 * held + n
            source = pl.ds(pl.multiple_of((spot % 4) * chunk, chunk), chunk)
            target = pl.ds(pl.multiple_of(((spot ^ (spot >> 1)) % 4) * chunk, chunk), chunk)
            e = dot(c_ref[...], w_ref[n * chunk:(n + 1) * chunk, :], 1, 1)
            a = a_ref[:, source].astype(jnp.float32)
            gate, sq = gate_of(a)
            slope = gate + (gate - gate * gate) * (a * (2 * GELU_A + 6 * GELU_B * sq))
            z_ref[:, target] = (e * slope).astype(jnp.bfloat16)


def act_grad_call(quarter, c, a, pieces, first, prior=None, tile=512):
    tokens, hidden = c.shape
    ffn = a.shape[1]
    row = lambda i, q: (i, 0)
    half = pl.BlockSpec((tile, ffn // 2), lambda i, q: (i, (q[0] ^ first) // 2))
    piece = pl.BlockSpec(pieces[0].shape, lambda i, q: (0, 0))
    extra = [] if prior is None else [pl.BlockSpec(memory_space=pl.ANY)]
    return pl.pallas_call(
        functools.partial(act_grad_kernel, first=first),
        grid_spec=pltpu.PrefetchScalarGridSpec(
            num_scalar_prefetch=1,
            grid=(tokens // tile,),
            in_specs=[pl.BlockSpec((tile, hidden), row), half, piece, piece] + extra,
            out_specs=half,
        ),
        out_shape=jax.ShapeDtypeStruct((tokens, ffn), jnp.bfloat16),
        input_output_aliases={} if prior is None else {5: 0},
        compiler_params=params(),
        cost_estimate=cost(tokens, hidden, ffn // 2, tokens * (2 * hidden + 2 * ffn) + hidden * ffn, tokens * ffn // 2),
    )(quarter, c, a, *pieces, *([] if prior is None else [prior]))


def in_grad_kernel(q_ref, z_ref, x_ref, c_ref, w0, w1, w2, w3, d_ref, v_ref):
    for rel, w_ref in enumerate((w0, w1, w2, w3)):
        width = w_ref.shape[0]
        cols = pl.ds(pl.multiple_of((q_ref[0] ^ rel) * width, width), width)
        v_ref[:, cols] = dot(z_ref[...], w_ref[...], 1, 1)
    v = lane_tiles(v_ref[...], RING_POS)
    x = x_ref[...].astype(jnp.float32)
    r = lax.rsqrt(jnp.mean(x * x, axis=-1, keepdims=True) + NORM_EPS)
    pull = r * v - x * (r * r * r * jnp.mean(x * v, axis=-1, keepdims=True))
    d_ref[...] = (c_ref[...].astype(jnp.float32) + pull).astype(jnp.bfloat16)


def in_grad_call(quarter, z, x, c, pieces, tile=512):
    tokens, hidden = x.shape
    ffn = z.shape[1]
    row = lambda i, q: (i, 0)
    piece = pl.BlockSpec(pieces[0].shape, lambda i, q: (0, 0))
    return pl.pallas_call(
        in_grad_kernel,
        grid_spec=pltpu.PrefetchScalarGridSpec(
            num_scalar_prefetch=1,
            grid=(tokens // tile,),
            in_specs=[pl.BlockSpec((tile, ffn), row), pl.BlockSpec((tile, hidden), row), pl.BlockSpec((tile, hidden), row)] + [piece] * 4,
            out_specs=pl.BlockSpec((tile, hidden), row),
            scratch_shapes=[pltpu.VMEM((tile, hidden), jnp.float32)],
        ),
        out_shape=jax.ShapeDtypeStruct((tokens, hidden), jnp.bfloat16),
        compiler_params=params(),
        cost_estimate=cost(tokens, hidden, ffn, 2 * tokens * (3 * hidden + ffn) + 2 * hidden * ffn),
    )(quarter, z, x, c, *pieces)


def after(value, event):
    return lax.optimization_barrier((value, event))[0]


def gather(shard):
    return lax.all_gather(shard, ALL_AXES, axis=0, tiled=True, axis_index_groups=GROUP)


def scatter_sum(total):
    return lax.psum_scatter(total, ALL_AXES, scatter_dimension=0, tiled=True, axis_index_groups=GROUP)


def regather(kept):
    twin = lax.ppermute(kept, ALL_AXES, TO_TWIN)
    own = lax.ppermute(kept, ALL_AXES, TO_PARTNER)
    last = lax.ppermute(twin, ALL_AXES, TO_PARTNER)
    return kept, own, twin, last


def solution(mesh):
    def body(tokens, cotangent, w_up, w_down):
        micro, per, hidden = tokens.shape
        layers = w_up.shape[0]
        ffn = w_up.shape[2]
        dev = lax.axis_index("local") * 4 + lax.axis_index("data")
        z_bit, y_bit, x_bit, core = dev // 8, (dev // 4) % 2, (dev // 2) % 2, dev % 2
        quarter = jnp.reshape(2 * jnp.where(x_bit == 1, z_bit, y_bit) + core, (1,)).astype(jnp.int32)

        x = tokens.reshape(micro * per, hidden)
        saved = []
        for layer in range(layers):
            if layer == 0:
                left = gather(w_up[layer][:, :ffn // 2])
                right = gather(w_up[layer][:, ffn // 2:])
                u, *prior = up_call(quarter, x, left, ffn)
                a, s, kept_up = up_call(quarter, u, right, ffn, 1, prior)
            else:
                u, a, s, kept_up = up_call(quarter, x, gather(w_up[layer]), ffn)
            x_next, kept_down = down_call(quarter, s, x, gather(w_down[layer]))
            saved.append((x, u, a, s, kept_up, kept_down))
            x = x_next
        out_x = x
        c = cotangent.reshape(micro * per, hidden)
        ups = [None] * layers
        downs = [None] * layers
        down_pieces = regather(after(saved[-1][-1], out_x))
        for layer in reversed(range(layers)):
            x_in, u, a, s, kept_up, kept_down = saved[layer]
            if layer == layers - 1:
                s = after(s, out_x)
            down_grad = weight_grad_call(s, c, 512, hidden, 512)
            downs[layer] = scatter_sum(down_grad)
            if layer == layers - 1:
                up_pieces = regather(after(kept_up, down_grad))
            z = act_grad_call(quarter, c, a, down_pieces[:2], 0)
            z = act_grad_call(quarter, c, a, down_pieces[2:], 2, z)
            if layer > 0:
                down_pieces = regather(after(saved[layer - 1][-1], z))
            up_grad = weight_grad_call(u, z, hidden, 512, 256)
            ups[layer] = scatter_sum(up_grad)
            c = in_grad_call(quarter, after(z, up_grad), x_in, c, up_pieces)
            if layer > 0:
                up_pieces = regather(after(saved[layer - 1][-2], c))
        return out_x.reshape(tokens.shape), c.reshape(tokens.shape), jnp.stack(ups), jnp.stack(downs)

    row_spec = P(None, ALL_AXES, None)
    return jax.shard_map(body, mesh=mesh, in_specs=(row_spec,) * 4, out_specs=(row_spec,) * 4, check_vma=False)
```

time: 1290 us -> 923 us (0.72)
  matrix products: 709 us -> 0 us
  Pallas kernels: 0 us -> 624 us
  waiting for transfers between devices: 426 us -> 252 us
  local copies, waits for them, and re-layouts: 83.6 us -> 13.3 us
  other arithmetic: 46.9 us -> 6.23 us
    dot_general x24 -> x0, matrix products: 709 us -> none  [the longest x4 185 us: layer_backward(): jnp.einsum('tm,fm->tf', d_out, down_mat, preferred_element_type=jnp.float32)]
    pallas_call x0 -> x15, Pallas kernels: none -> 624 us  [the longest x4 170 us: weight_grad_call(): pl.pallas_call(functools.partial(weight_grad_kernel, chunk=chunk), grid=(...]
    reduce_scatter x4, waiting for transfers between devices: 259 us -> 7.24 us  [scatter_sum(): lax.psum_scatter(total, ALL_AXES, scatter_dimension=0, tiled=True, axis_i...]
    ppermute x0 -> x12, waiting for transfers between devices: none -> 185 us  [the longest x4 183 us: regather(): twin = lax.ppermute(kept, ALL_AXES, TO_TWIN)]
    all_gather x8 -> x5, waiting for transfers between devices: 166 us -> 57.3 us  [gather(): lax.all_gather(shard, ALL_AXES, axis=0, tiled=True, axis_index_groups=GROUP)]
    unnamed x72 -> x16, local copies, waits for them, and re-layouts: 54.3 us -> 9.24 us
    another operation x6 -> x2, other arithmetic: 31.6 us -> 6.23 us  [the longest x1 3.17 us: body(): jnp.stack(downs)]
  transfers between devices with their start and end apart: 12 -> 21, of which waited for: 6 -> 10; matrix products, arithmetic and copies ran while one was open for 65% -> 0% of each run, Pallas kernels for 0% -> 59%
where the time goes in v1:
time: 923 us; the launch traced here: 916 us
  Pallas kernels  624 us (68%)
  waiting for transfers between devices  252 us (27%)
  between operations  14.2 us (2%)
  local copies, waits for them, and re-layouts  13.3 us (1%)
    ppermute x4, waiting for transfers between devices, regather(): twin = lax.ppermute(kept, ALL_AXES, TO_TWIN)  183 us
    pallas_call x4, Pallas kernels, weight_grad_call(): pl.pallas_call(functools.partial(weight_grad_kernel, chunk=chunk), grid=(...  170 us
    pallas_call x4, Pallas kernels, act_grad_call(): pl.pallas_call(functools.partial(act_grad_kernel, first=first), grid_spec...  145 us
    pallas_call x3, Pallas kernels, up_call(): pl.pallas_call(functools.partial(up_kernel, normalize=fresh, chunk=ffn //...  126 us
    pallas_call x2, Pallas kernels, in_grad_call(): pl.pallas_call(in_grad_kernel, grid_spec=pltpu.PrefetchScalarGridSpec(num...  98 us
    pallas_call x2, Pallas kernels, down_call(): pl.pallas_call(functools.partial(down_kernel, chunk=chunk), grid_spec=plt...  85.9 us
    all_gather x5, waiting for transfers between devices, gather(): lax.all_gather(shard, ALL_AXES, axis=0, tiled=True, axis_index_groups=GROUP)  57.3 us
  transfers between devices with their start and end apart: 21, of which 10 were waited for; matrix products, arithmetic and copies ran while one was open for 0% of the time, Pallas kernels for 59%

profile of v1, /device:TPU:0, one launch (start us, length us, event | category | flops | bytes accessed | tf_op | source)
XLA Modules:
  0.0 916.2 jit_solution(6784840655899048274)
XLA Ops:
  7.2 0.0 all-gather.9.cloned.1.call-start
  7.2 2.2 fusion.1
  9.4 0.8 fusion.2
  10.2 0.0 all-gather.9.cloned.1.call-update
  10.2 0.0 all-gather.11.cloned.1.call-start
  10.3 0.7 all-gather.11.cloned.1.call-update
  11.0 0.0 all-gather.13.cloned.1.call-start
  11.0 1.0 fusion
  12.1 0.0 all-gather.13.cloned.1.call-update
  12.1 0.0 all-gather.15.cloned.1.call-start
  12.1 0.5 all-gather.15.cloned.1.call-update
  12.7 0.0 all-gather.17.cloned.1.call-start
  12.7 0.5 all-gather.17.cloned.1.call-update
  13.3 0.0 reduce-scatter.11.cloned.1.call-start
  13.4 32.5 %all-gather.9.cloned.1.call-done.w_ref = bf16[1024,2048]{1,0:T(8,128)(2,1)} async-done(((bf16[64,2048]{1,0:T(8,128)(2,1)}), bf16[1024,2048]{1,0:T(8,128)(2,1)}) %all-gather.9.cloned.1.call-update) | async-done | bytes 4194320 | tf_op jit(solution)/shard_map/all_gather | solution.py:227
  45.9 33.2 %up.3 = (bf16[4096,1024]{1,0:T(8,128)(2,1)}, bf16[4096,4096]{1,0:T(8,128)(2,1)}, bf16[4096,4096]{1,0:T(8,128)(2,1)}, bf16[256,4096]{1,0:T(8,128)(2,1)}) custom-call(s32[1]{0:T(128)} %bitcast.q_ref, bf16[4096,1024]{1,0:T(8,128)(2,1)} %bitcast.22, bf16[1024,2048]{1,0:T(8,128)(2,1)} %all-gather.9.cloned.1.call-done.w_ref), custom_call_target="tpu_custom_call" | custom-call | flops 17179869184 | bytes 54525952 | tf_op jit(solution)/shard_map/up/pallas_call | solution.py:85
  79.1 0.5 all-gather.11.cloned.1.call-done.w_ref
  79.6 31.7 %up.4 = (bf16[4096,4096]{1,0:T(8,128)(2,1)}, bf16[4096,4096]{1,0:T(8,128)(2,1)}, bf16[256,4096]{1,0:T(8,128)(2,1)}) custom-call(s32[1]{0:T(128)} %bitcast.q_ref, bf16[4096,1024]{1,0:T(8,128)(2,1)} %get-tuple-element.26.in_ref.l_ref, ...), custom_call_target="tpu_custom_call", output_to_operand_aliasing={{0}: (3, {}), {1}: (4, {}), {2}: (5, {})} | custom-call | flops 17179869184 | bytes 54525952 | tf_op jit(solution)/shard_map/up/pallas_call | solution.py:85
  111.2 17.5 %all-gather.13.cloned.1.call-done = bf16[1,4096,1024]{2,1,0:T(8,128)(2,1)} async-done(((bf16[1,256,1024]{2,1,0:T(8,128)(2,1)}), bf16[1,4096,1024]{2,1,0:T(8,128)(2,1)}) %all-gather.13.cloned.1.call-update) | async-done | bytes 8388624 | tf_op jit(solution)/shard_map/all_gather | solution.py:227
  128.7 42.9 %down.2 = (bf16[4096,1024]{1,0:T(8,128)(2,1)}, bf16[1024,1024]{1,0:T(8,128)(2,1)}) custom-call(s32[1]{0:T(128)} %bitcast.q_ref, bf16[4096,4096]{1,0:T(8,128)(2,1)} %get-tuple-element.30.s_ref.l_ref, bf16[4096,1024]{1,0:T(8,128)(2,1)} %bitcast.23, bf16[4096,1024]{1,0:T(8,128)(2,1)} %bitcast.25), custom_call_target="tpu_custom_call" | custom-call | flops 34359738368 | bytes 58720256 | tf_op jit(solution)/shard_map/down/pallas_call | solution.py:114
  171.6 6.8 all-gather.15.cloned.1.call-done
  178.4 60.9 %up.5 = (bf16[4096,1024]{1,0:T(8,128)(2,1)}, bf16[4096,4096]{1,0:T(8,128)(2,1)}, bf16[4096,4096]{1,0:T(8,128)(2,1)}, bf16[256,4096]{1,0:T(8,128)(2,1)}) custom-call(s32[1]{0:T(128)} %bitcast.q_ref, bf16[4096,1024]{1,0:T(8,128)(2,1)} %get-tuple-element.31.in_ref.x_ref, bf16[1024,4096]{1,0:T(8,128)(2,1)} %bitcast.26), custom_call_target="tpu_custom_call" | custom-call | flops 34359738368 | bytes 92274688 | tf_op jit(solution)/shard_map/up/pallas_call | solution.py:85
  239.3 0.0 all-gather.17.cloned.1.call-done
  239.3 43.0 %down.3 = (bf16[4096,1024]{1,0:T(8,128)(2,1)}, bf16[1024,1024]{1,0:T(8,128)(2,1)}) custom-call(s32[1]{0:T(128)} %bitcast.q_ref, bf16[4096,4096]{1,0:T(8,128)(2,1)} %get-tuple-element.40.s_ref.l_ref, bf16[4096,1024]{1,0:T(8,128)(2,1)} %get-tuple-element.31.in_ref.x_ref, bf16[4096,1024]{1,0:T(8,128)(2,1)} %bitcast.27), custom_call_target="tpu_custom_call" | custom-call | flops 34359738368 | bytes 58720256 | tf_op jit(solution)/shard_map/down/pallas_call | solution.py:114
  282.3 42.2 %shard_map.78 = f32[4096,1024]{1,0:T(8,128)} custom-call(bf16[4096,4096]{1,0:T(8,128)(2,1)} %get-tuple-element.40.s_ref.l_ref, bf16[4096,1024]{1,0:T(8,128)(2,1)} %bitcast.14), custom_call_target="tpu_custom_call" | custom-call | flops 34359738368 | bytes 58720256 | tf_op jit(solution)/shard_map/pallas_call | solution.py:141
  324.5 0.0 reduce-scatter.11.cloned.1.call-update
  324.5 0.0 reduce-scatter.9.cloned.1.call-start
  324.6 1.5 copy-done.1
  326.1 1.4 collective-permute-start
  327.5 0.6 collective-permute-start.4
  328.1 46.6 %collective-permute-done.w0 = bf16[1024,1024]{1,0:T(8,128)(2,1)} collective-permute-done((bf16[1024,1024]{1,0:T(8,128)(2,1)S(1)}, bf16[1024,1024]{1,0:T(8,128)(2,1)}, u32[]{:S(2)}, u32[]{:S(2)}) %collective-permute-start) | collective-permute-done | bytes 2097184 | tf_op jit(solution)/shard_map/ppermute | solution.py:235
  374.7 0.5 collective-permute-start.3
  375.2 43.7 %collective-permute-done.4.w2 = bf16[256,4096]{1,0:T(8,128)(2,1)} collective-permute-done((bf16[256,4096]{1,0:T(8,128)(2,1)}, bf16[256,4096]{1,0:T(8,128)(2,1)}, u32[]{:S(2)}, u32[]{:S(2)}) %collective-permute-start.4) | collective-permute-done | bytes 2097184 | tf_op jit(solution)/shard_map/ppermute | solution.py:235
  418.9 1.4 copy-done.2
  420.3 36.2 %shard_map.75.refs_0_ = bf16[4096,4096]{1,0:T(8,128)(2,1)} custom-call(s32[1]{0:T(128)} %bitcast.q_ref, bf16[4096,1024]{1,0:T(8,128)(2,1)} %bitcast.15, bf16[4096,4096]{1,0:T(8,128)(2,1)} %get-tuple-element.34.a_ref, bf16[1024,1024]{1,0:T(8,128)(2,1)} %get-tuple-element.36.w0, bf16[1024,1024]{1,0:T(8,128)(2,1)} %copy-done.2), custom_call_target="tpu_custom_call" | custom-call | flops 17179869184 | bytes 46137344 | tf_op jit(solution)/shard_map/pallas_call | solution.py:175
  456.5 36.0 %shard_map.76.r_ref.z_ref = bf16[4096,4096]{1,0:T(8,128)(2,1)} custom-call(s32[1]{0:T(128)} %bitcast.q_ref, bf16[4096,1024]{1,0:T(8,128)(2,1)} %bitcast.16, bf16[4096,4096]{1,0:T(8,128)(2,1)} %get-tuple-element.34.a_ref, bf16[1024,1024]{1,0:T(8,128)(2,1)} %collective-permute-done.w0, ...), custom_call_target="tpu_custom_call", output_to_operand_aliasing={{}: (5, {})} | custom-call | flops 17179869184 | bytes 46137344 | tf_op jit(solution)/shard_map/pallas_call | solution.py:175
  492.6 42.4 %shard_map.77 = f32[1024,4096]{1,0:T(8,128)} custom-call(bf16[4096,1024]{1,0:T(8,128)(2,1)} %get-tuple-element.37.l_ref, bf16[4096,4096]{1,0:T(8,128)(2,1)} %shard_map.76.r_ref.z_ref), custom_call_target="tpu_custom_call" | custom-call | flops 34359738368 | bytes 58720256 | tf_op jit(solution)/shard_map/pallas_call | solution.py:141
  535.0 49.0 %shard_map.79.c_ref.r_ref = bf16[4096,1024]{1,0:T(8,128)(2,1)} custom-call(s32[1]{0:T(128)} %bitcast.q_ref, bf16[4096,4096]{1,0:T(8,128)(2,1)} %shard_map.76.r_ref.z_ref, bf16[4096,1024]{1,0:T(8,128)(2,1)} %get-tuple-element.31.in_ref.x_ref, bf16[4096,1024]{1,0:T(8,128)(2,1)} %bitcast.17, bf16[256,4096]{1,0:T(8,128)(2,1)} %get-tuple-element.41.w0, ...), custom_call_target="tpu_custom_call" | custom-call | flops 34359738368 | bytes 67108864 | tf_op jit(solution)/shard_map/pallas_call | solution.py:207
  584.0 42.3 %shard_map.84 = f32[4096,1024]{1,0:T(8,128)} custom-call(bf16[4096,4096]{1,0:T(8,128)(2,1)} %get-tuple-element.30.s_ref.l_ref, bf16[4096,1024]{1,0:T(8,128)(2,1)} %shard_map.79.c_ref.r_ref), custom_call_target="tpu_custom_call" | custom-call | flops 34359738368 | bytes 58720256 | tf_op jit(solution)/shard_map/pallas_call | solution.py:141
  626.3 0.0 reduce-scatter.9.cloned.1.call-update
  626.3 0.0 copy-start
  626.3 0.0 reduce-scatter.7.cloned.1.call-start
  626.4 0.7 reduce-scatter.7.cloned.1.call-update
  627.1 0.0 reduce-scatter.5.cloned.1.call-start
  627.1 0.8 copy-done
  627.9 1.3 collective-permute-start.6
  629.2 0.2 collective-permute-start.8
  629.4 46.6 %collective-permute-done.6.w0 = bf16[1024,1024]{1,0:T(8,128)(2,1)} collective-permute-done((bf16[1024,1024]{1,0:T(8,128)(2,1)S(1)}, bf16[1024,1024]{1,0:T(8,128)(2,1)}, u32[]{:S(2)}, u32[]{:S(2)}) %collective-permute-start.6) | collective-permute-done | bytes 2097184 | tf_op jit(solution)/shard_map/ppermute | solution.py:235
  676.0 1.3 copy-done.4
  677.3 36.3 %shard_map.80.refs_0_ = bf16[4096,4096]{1,0:T(8,128)(2,1)} custom-call(s32[1]{0:T(128)} %bitcast.q_ref, bf16[4096,1024]{1,0:T(8,128)(2,1)} %shard_map.79.c_ref.r_ref, bf16[4096,4096]{1,0:T(8,128)(2,1)} %get-tuple-element.42.a_ref, bf16[1024,1024]{1,0:T(8,128)(2,1)} %get-tuple-element.44.w0, bf16[1024,1024]{1,0:T(8,128)(2,1)} %copy-done.4), custom_call_target="tpu_custom_call" | custom-call | flops 17179869184 | bytes 46137344 | tf_op jit(solution)/shard_map/pallas_call | solution.py:175
  713.6 36.1 %shard_map.81.r_ref.z_ref = bf16[4096,4096]{1,0:T(8,128)(2,1)} custom-call(s32[1]{0:T(128)} %bitcast.q_ref, bf16[4096,1024]{1,0:T(8,128)(2,1)} %shard_map.79.c_ref.r_ref, bf16[4096,4096]{1,0:T(8,128)(2,1)} %get-tuple-element.42.a_ref, bf16[1024,1024]{1,0:T(8,128)(2,1)} %collective-permute-done.6.w0, ...), custom_call_target="tpu_custom_call", output_to_operand_aliasing={{}: (5, {})} | custom-call | flops 17179869184 | bytes 46137344 | tf_op jit(solution)/shard_map/pallas_call | solution.py:175
  749.7 42.7 %shard_map.82 = f32[1024,4096]{1,0:T(8,128)} custom-call(bf16[4096,1024]{1,0:T(8,128)(2,1)} %get-tuple-element.26.in_ref.l_ref, bf16[4096,4096]{1,0:T(8,128)(2,1)} %shard_map.81.r_ref.z_ref), custom_call_target="tpu_custom_call" | custom-call | flops 34359738368 | bytes 58720256 | tf_op jit(solution)/shard_map/pallas_call | solution.py:141
  792.5 0.0 reduce-scatter.5.cloned.1.call-update
  792.5 1.6 copy-done.3
  794.1 1.4 collective-permute-start.10
  795.4 0.2 collective-permute-start.9
  795.7 46.4 %collective-permute-done.10.w2 = bf16[256,4096]{1,0:T(8,128)(2,1)S(1)} collective-permute-done((bf16[256,4096]{1,0:T(8,128)(2,1)S(1)}, bf16[256,4096]{1,0:T(8,128)(2,1)S(1)}, u32[]{:S(2)}, u32[]{:S(2)}) %collective-permute-start.10) | collective-permute-done | bytes 2097184 | tf_op jit(solution)/shard_map/ppermute | solution.py:235
  842.0 1.3 copy-done.6
  843.4 1.3 copy-done.7
  844.7 2.2 collective-permute-done.11.w3
  846.9 49.0 %shard_map.83 = bf16[4096,1024]{1,0:T(8,128)(2,1)} custom-call(s32[1]{0:T(128)} %bitcast.q_ref, bf16[4096,4096]{1,0:T(8,128)(2,1)} %shard_map.81.r_ref.z_ref, bf16[4096,1024]{1,0:T(8,128)(2,1)} %bitcast.24, bf16[4096,1024]{1,0:T(8,128)(2,1)} %shard_map.79.c_ref.r_ref, bf16[256,4096]{1,0:T(8,128)(2,1)} %get-tuple-element.47.w0, bf16[256,4096]{1,0:T(8,128)(2,1)} %copy-done.7, ...), custom_call_target="tpu_custom_call" | custom-call | flops 34359738368 | bytes 67108864 | tf_op jit(solution)/shard_map/pallas_call | solution.py:207
  895.9 3.2 pad_maximum_fusion.1
  899.1 7.2 reduce-scatter.5.cloned.1.call-done
  906.4 3.1 pad_maximum_fusion
  (23 shorter events, 0.1 us)
Async XLA Ops:
  7.2 3.9 copy-start.5
  7.2 38.7 %all-gather.9.cloned.1.call-start = ((), (), s32[]{:S(2)}) async-start(), calls=%async_computation.4 | async-start | bytes 4456448 | tf_op jit(solution)/shard_map/all_gather | solution.py:227
  10.2 69.4 %all-gather.11.cloned.1.call-start = ((), (), s32[]{:S(2)}) async-start(), calls=%async_computation.5 | async-start | bytes 4456448 | tf_op jit(solution)/shard_map/all_gather | solution.py:227
  11.0 117.7 %all-gather.13.cloned.1.call-start = ((), (), s32[]{:S(2)}) async-start(), calls=%async_computation.10 | async-start | bytes 8912896 | tf_op jit(solution)/shard_map/all_gather | solution.py:227
  12.1 166.3 %all-gather.15.cloned.1.call-start = ((), (), s32[]{:S(2)}) async-start(), calls=%async_computation.11 | async-start | bytes 8912896 | tf_op jit(solution)/shard_map/all_gather | solution.py:227
  12.7 226.6 %all-gather.17.cloned.1.call-start = ((), (), s32[]{:S(2)}) async-start(), calls=%async_computation.12 | async-start | bytes 8912896 | tf_op jit(solution)/shard_map/all_gather | solution.py:227
  13.3 882.7 %reduce-scatter.11.cloned.1.call-start = ((), (), s32[]{:S(2)}) async-start(), calls=%async_computation.9 | async-start | bytes 17825792 | tf_op jit(solution)/shard_map/reduce_scatter | solution.py:231
  324.5 1.6 copy-start.1
  324.5 571.4 %reduce-scatter.9.cloned.1.call-start = ((), (), s32[]{:S(2)}) async-start(), calls=%async_computation.8 | async-start | bytes 17825792 | tf_op jit(solution)/shard_map/reduce_scatter | solution.py:231
  326.1 48.6 %collective-permute-start = (bf16[1024,1024]{1,0:T(8,128)(2,1)S(1)}, bf16[1024,1024]{1,0:T(8,128)(2,1)}, u32[]{:S(2)}, u32[]{:S(2)}) collective-permute-start(bf16[1024,1024]{1,0:T(8,128)(2,1)S(1)} %copy-done.1), channel_id=1, source_target_pairs={{0,4},{1,5},{2,10},{3,11},{4,0},{5,1},{6,14},{7,15},{8,12},{9,13},... | collective-permute-start | bytes 6291464 | tf_op jit(solution)/shard_map/ppermute | solution.py:235
  327.5 91.4 %collective-permute-start.4 = (bf16[256,4096]{1,0:T(8,128)(2,1)}, bf16[256,4096]{1,0:T(8,128)(2,1)}, u32[]{:S(2)}, u32[]{:S(2)}) collective-permute-start(bf16[256,4096]{1,0:T(8,128)(2,1)} %get-tuple-element.41.w0), channel_id=1, source_target_pairs={{0,4},{1,5},{2,10},{3,11},{4,0},{5,1},{6,14},{7,15},{8,12},{9,13},... | collective-permute-start | bytes 6291464 | tf_op jit(solution)/shard_map/ppermute | solution.py:235
  328.1 90.8 %collective-permute-start.2 = (bf16[1024,1024]{1,0:T(8,128)(2,1)S(1)}, bf16[1024,1024]{1,0:T(8,128)(2,1)S(1)}, u32[]{:S(2)}, u32[]{:S(2)}) collective-permute-start(bf16[1024,1024]{1,0:T(8,128)(2,1)S(1)} %copy-done.1), channel_id=1, source_target_pairs={{0,1},{1,0},{2,3},{3,2},{4,5},{5,4},{6,7},{7,6},{8,9},{9,8},{10,11... | collective-permute-start | bytes 6291464 | tf_op jit(solution)/shard_map/ppermute | solution.py:236
  374.7 81.9 %collective-permute-start.1 = (bf16[1024,1024]{1,0:T(8,128)(2,1)}, bf16[1024,1024]{1,0:T(8,128)(2,1)}, u32[]{:S(2)}, u32[]{:S(2)}) collective-permute-start(bf16[1024,1024]{1,0:T(8,128)(2,1)} %collective-permute-done.w0), channel_id=1, source_target_pairs={{0,1},{1,0},{2,3},{3,2},{4,5},{5,4},{6,7},{7,6},{8,9},{9,8},{10,11... | collective-permute-start | bytes 6291464 | tf_op jit(solution)/shard_map/ppermute | solution.py:237
  374.7 160.3 %collective-permute-start.3 = (bf16[256,4096]{1,0:T(8,128)(2,1)}, bf16[256,4096]{1,0:T(8,128)(2,1)}, u32[]{:S(2)}, u32[]{:S(2)}) collective-permute-start(bf16[256,4096]{1,0:T(8,128)(2,1)} %get-tuple-element.41.w0), channel_id=1, source_target_pairs={{0,1},{1,0},{2,3},{3,2},{4,5},{5,4},{6,7},{7,6},{8,9},{9,8},{10,11... | collective-permute-start | bytes 6291464 | tf_op jit(solution)/shard_map/ppermute | solution.py:236
  418.9 116.1 %collective-permute-start.5 = (bf16[256,4096]{1,0:T(8,128)(2,1)}, bf16[256,4096]{1,0:T(8,128)(2,1)}, u32[]{:S(2)}, u32[]{:S(2)}) collective-permute-start(bf16[256,4096]{1,0:T(8,128)(2,1)} %collective-permute-done.4.w2), channel_id=1, source_target_pairs={{0,1},{1,0},{2,3},{3,2},{4,5},{5,4},{6,7},{7,6},{8,9},{9,8},{10,11... | collective-permute-start | bytes 6291464 | tf_op jit(solution)/shard_map/ppermute | solution.py:237
  418.9 1.4 copy-start.2
  626.3 1.6 copy-start
  626.3 272.8 %reduce-scatter.7.cloned.1.call-start = ((), (), s32[]{:S(2)}) async-start(), calls=%async_computation.7 | async-start | bytes 17825792 | tf_op jit(solution)/shard_map/reduce_scatter | solution.py:231
  627.1 279.3 %reduce-scatter.5.cloned.1.call-start = ((), (), s32[]{:S(2)}) async-start(), calls=%async_computation.6 | async-start | bytes 17825792 | tf_op jit(solution)/shard_map/reduce_scatter | solution.py:231
  627.9 48.0 %collective-permute-start.6 = (bf16[1024,1024]{1,0:T(8,128)(2,1)S(1)}, bf16[1024,1024]{1,0:T(8,128)(2,1)}, u32[]{:S(2)}, u32[]{:S(2)}) collective-permute-start(bf16[1024,1024]{1,0:T(8,128)(2,1)S(1)} %copy-done), channel_id=1, source_target_pairs={{0,4},{1,5},{2,10},{3,11},{4,0},{5,1},{6,14},{7,15},{8,12},{9,13},... | collective-permute-start | bytes 6291464 | tf_op jit(solution)/shard_map/ppermute | solution.py:235
  629.2 46.8 %collective-permute-start.8 = (bf16[1024,1024]{1,0:T(8,128)(2,1)S(1)}, bf16[1024,1024]{1,0:T(8,128)(2,1)S(1)}, u32[]{:S(2)}, u32[]{:S(2)}) collective-permute-start(bf16[1024,1024]{1,0:T(8,128)(2,1)S(1)} %copy-done), channel_id=1, source_target_pairs={{0,1},{1,0},{2,3},{3,2},{4,5},{5,4},{6,7},{7,6},{8,9},{9,8},{10,11... | collective-permute-start | bytes 6291464 | tf_op jit(solution)/shard_map/ppermute | solution.py:236
  675.9 37.7 %collective-permute-start.7 = (bf16[1024,1024]{1,0:T(8,128)(2,1)}, bf16[1024,1024]{1,0:T(8,128)(2,1)}, u32[]{:S(2)}, u32[]{:S(2)}) collective-permute-start(bf16[1024,1024]{1,0:T(8,128)(2,1)} %collective-permute-done.6.w0), channel_id=1, source_target_pairs={{0,1},{1,0},{2,3},{3,2},{4,5},{5,4},{6,7},{7,6},{8,9},{9,8},{10,11... | collective-permute-start | bytes 6291464 | tf_op jit(solution)/shard_map/ppermute | solution.py:237
  676.0 1.3 copy-start.4
  792.5 1.6 copy-start.3
  794.1 48.0 %collective-permute-start.10 = (bf16[256,4096]{1,0:T(8,128)(2,1)S(1)}, bf16[256,4096]{1,0:T(8,128)(2,1)S(1)}, u32[]{:S(2)}, u32[]{:S(2)}) collective-permute-start(bf16[256,4096]{1,0:T(8,128)(2,1)S(1)} %copy-done.3), channel_id=1, source_target_pairs={{0,4},{1,5},{2,10},{3,11},{4,0},{5,1},{6,14},{7,15},{8,12},{9,13},... | collective-permute-start | bytes 6291464 | tf_op jit(solution)/shard_map/ppermute | solution.py:235
  795.4 46.6 %collective-permute-start.9 = (bf16[256,4096]{1,0:T(8,128)(2,1)S(1)}, bf16[256,4096]{1,0:T(8,128)(2,1)S(1)}, u32[]{:S(2)}, u32[]{:S(2)}) collective-permute-start(bf16[256,4096]{1,0:T(8,128)(2,1)S(1)} %copy-done.3), channel_id=1, source_target_pairs={{0,1},{1,0},{2,3},{3,2},{4,5},{5,4},{6,7},{7,6},{8,9},{9,8},{10,11... | collective-permute-start | bytes 6291464 | tf_op jit(solution)/shard_map/ppermute | solution.py:236
  842.0 1.3 copy-start.6
  842.0 4.9 collective-permute-start.11
  843.4 1.3 copy-start.7
Sparse Core Ops, SparseCore 0:
  10.3 35.5 all-gather.8
  47.5 32.0 all-gather.10
  81.7 46.9 all-gather.12
  130.7 47.6 all-gather.14
  179.8 47.6 all-gather.16
  324.6 91.7 reduce-scatter.10
  626.4 91.7 reduce-scatter.8
  720.4 91.7 reduce-scatter.6
  814.5 91.8 reduce-scatter.4
